TPU v7x, 32 devices: a whole 2x2x4 slice. The times are simulated.
32 devices in a mesh: grp: 4 (over y, x), slab: 8 (over z, core).
Axes of the slice: x: 2, y: 2, z: 4, core: 2. Of those that a mesh axis runs over, the one named last changes fastest.
Arguments:
- state: float32 [4, 2, 256, 128, 256], P(None, None, 'grp', 'slab'), may hold values from -5.6 to 5.6
- kz_group: int32 [256], replicated, may hold values from 0 to 7, as said below
- cutoffs: int32 [3], replicated, may hold values from 28 to 32
- damping: float32 [8], replicated, may hold values from 0.005 to 0.5
- power: float32 [8], replicated, may hold values from 0.2 to 4
Outputs:
- new_state: float32 [4, 2, 256, 128, 256], P(None, None, 'grp', 'slab')
Inputs may be any that keep to these rules, and one draw needn't show every extreme that they name: `kz_group`: each of the 8 groups holds exactly 32 indices.
All inputs are finite; a program needn't handle non-finite values.
Results may differ from a plain program's by a relative error of at most 0.00005.
Values sent between devices are 32-bit elements; how exact they have to be, the bound alone decides.
A program may use at most 192 MiB of HBM per device.

v0:
```python
import math
import jax
import jax.numpy as jnp
from jax import lax
from jax.sharding import PartitionSpec as P

NX = 256
NY = 256
NZ = 256
GROUPS = 8
KX = 128
GMODES = 32
PRECISE = lax.Precision.HIGHEST
TWO_PI = 6.283185307179586
TIME_STEP = 0.25
CORIOLIS = 1.0
BRUNT_SQUARED = 2.0
EPSILON = 1e-06


def signed(index, length):
    return jnp.where(index < length // 2, index, index - length)


def angles(modes, points, length):
    phase = modes[:, None] * points[None, :] % length
    theta = phase.astype(jnp.float32) * (TWO_PI / length)
    return (jnp.cos(theta), jnp.sin(theta))


def rotate(pattern, real_part, imag_part, cosine_table, sine_table, forward):
    first = jnp.einsum(pattern, real_part, cosine_table, precision=PRECISE)
    second = jnp.einsum(pattern, imag_part, sine_table, precision=PRECISE)
    third = jnp.einsum(pattern, real_part, sine_table, precision=PRECISE)
    fourth = jnp.einsum(pattern, imag_part, cosine_table, precision=PRECISE)
    if forward:
        return (first + second, fourth - third)
    return (first - second, third + fourth)


def times_i(entries):
    return jnp.stack([-entries[1], entries[0]])


def x_forward(products, pattern, cosine_table, sine_table):
    real_x = jnp.einsum(pattern, products, cosine_table, precision=PRECISE)
    imag_x = -jnp.einsum(pattern, products, sine_table, precision=PRECISE)
    return (real_x, imag_x)


def shards(state, kz_group, cutoffs, damping, power):
    grp_count = lax.axis_size("grp")
    grp_index = lax.axis_index("grp")
    slab_index = lax.axis_index("slab")
    slots_here = state.shape[2]
    cols_here = state.shape[3]
    groups_here = GROUPS // grp_count
    normalizer = 1.0 / math.sqrt(NX * NY * NZ)
    slot_mode = jnp.argsort(kz_group, stable=True)
    local_mode = lax.dynamic_slice_in_dim(slot_mode, grp_index * slots_here, slots_here)
    mode_z = signed(local_mode, NZ)
    mode_x = slab_index * cols_here + jnp.arange(cols_here, dtype=jnp.int32)
    mode_y = signed(jnp.arange(NY, dtype=jnp.int32), NY)
    wave_z = (TWO_PI / NZ * mode_z.astype(jnp.float32))[:, None, None]
    wave_x = (TWO_PI / NX * mode_x.astype(jnp.float32))[None, :, None]
    wave_y = (TWO_PI / NY * mode_y.astype(jnp.float32))[None, None, :]
    flow_x, flow_y, flow_z, buoyant = (state[0], state[1], state[2], state[3])
    means = None
    swirl_x = times_i(wave_y * flow_z - wave_z * flow_y)
    swirl_y = times_i(wave_z * flow_x - wave_x * flow_z)
    swirl_z = times_i(wave_x * flow_y - wave_y * flow_x)
    fields = jnp.stack([flow_x, flow_y, flow_z, buoyant, swirl_x, swirl_y, swirl_z])
    cosine_y, sine_y = angles(jnp.arange(NY, dtype=jnp.int32), jnp.arange(NY, dtype=jnp.int32), NY)
    real_y, imag_y = rotate("fzxm,my->fzxy", fields[:, 0], fields[:, 1], cosine_y, sine_y, False)
    spectral_y = jnp.stack([real_y, imag_y], axis=1)
    cosine_zi, sine_zi = angles(slot_mode, jnp.arange(NZ, dtype=jnp.int32), NZ)
    cosine_zf, sine_zf = angles(jnp.arange(NZ, dtype=jnp.int32), slot_mode, NZ)
    weights = jnp.where(jnp.arange(KX) == 0, 1.0, 2.0).astype(jnp.float32) * normalizer
    cosine_x, sine_x = angles(jnp.arange(KX, dtype=jnp.int32), jnp.arange(NX, dtype=jnp.int32), NX)
    cosine_x = cosine_x * weights[:, None]
    sine_x = sine_x * weights[:, None]
    cosine_xf, sine_xf = angles(
        jnp.arange(NX, dtype=jnp.int32), jnp.arange(KX, dtype=jnp.int32), NX
    )
    pieces = lax.all_to_all(spectral_y, "grp", split_axis=4, concat_axis=2, tiled=True)
    real_part, imag_part = rotate(
        "fsxy,sz->fzxy", pieces[:, 0], pieces[:, 1], cosine_zi, sine_zi, False
    )
    grid_z = jnp.stack([real_part, imag_part], axis=1)
    pieces = lax.all_to_all(grid_z, "slab", split_axis=2, concat_axis=3, tiled=True)
    physical = jnp.einsum("fzky,kn->fzyn", pieces[:, 0], cosine_x, precision=PRECISE) - jnp.einsum(
        "fzky,kn->fzyn", pieces[:, 1], sine_x, precision=PRECISE
    )
    grid_u = physical[0]
    grid_v = physical[1]
    grid_w = physical[2]
    grid_b = physical[3]
    grid_ox = physical[4]
    grid_oy = physical[5]
    grid_oz = physical[6]
    products = jnp.stack(
        [
            grid_v * grid_oz - grid_w * grid_oy,
            grid_w * grid_ox - grid_u * grid_oz,
            grid_u * grid_oy - grid_v * grid_ox,
            grid_u * grid_b,
            grid_v * grid_b,
            grid_w * grid_b,
        ]
    )
    real_x, imag_x = x_forward(products, "fzyn,nk->fzky", cosine_xf, sine_xf)
    sectioned = jnp.stack([real_x, imag_x], axis=1)
    pieces = lax.all_to_all(sectioned, "slab", split_axis=3, concat_axis=2, tiled=True)
    real_part, imag_part = rotate(
        "fzxy,zs->fsxy", pieces[:, 0], pieces[:, 1], cosine_zf, sine_zf, True
    )
    spectral_z = jnp.stack([real_part, imag_part], axis=1)
    pieces = lax.all_to_all(spectral_z, "grp", split_axis=2, concat_axis=4, tiled=True)
    real_part, imag_part = rotate(
        "fsxy,ym->fsxm", pieces[:, 0], pieces[:, 1], cosine_y, sine_y, True
    )
    tendency = jnp.stack([real_part, imag_part], axis=1) * normalizer
    real_part = state[:, 0]
    imag_part = state[:, 1]
    cell_flux = real_part[2] * real_part[3] + imag_part[2] * imag_part[3]
    cell_energy = 0.5 * (
        jnp.sum(real_part[:3] ** 2 + imag_part[:3] ** 2, axis=0)
        + (real_part[3] ** 2 + imag_part[3] ** 2) / BRUNT_SQUARED
    )
    partial_value = jnp.stack(
        [jnp.sum(cell_flux, axis=(1, 2)), jnp.sum(cell_energy, axis=(1, 2))], axis=1
    )
    partial_value = jnp.sum(partial_value.reshape(groups_here, GMODES, 2), axis=1)
    totals = lax.psum(partial_value, "slab")
    means = totals / (GMODES * KX * NY)
    kept = (
        (96 * jnp.abs(mode_z) <= cutoffs[2] * NZ)[:, None, None]
        & (96 * mode_x <= cutoffs[0] * NX)[None, :, None]
        & (96 * jnp.abs(mode_y) <= cutoffs[1] * NY)[None, None, :]
    ).astype(jnp.float32)
    moment_x, moment_y, moment_z = (tendency[0] * kept, tendency[1] * kept, tendency[2] * kept)
    divergence = wave_x * tendency[3] + wave_y * tendency[4] + wave_z * tendency[5]
    source_b = jnp.stack([divergence[1], -divergence[0]]) * kept
    power_here = lax.dynamic_slice_in_dim(power, grp_index * groups_here, groups_here)
    damping_here = lax.dynamic_slice_in_dim(damping, grp_index * groups_here, groups_here)
    forcing = (power_here - means[:, 0]) / (2.0 * (means[:, 1] + EPSILON))
    forcing_slot = jnp.repeat(forcing, GMODES)[:, None, None]
    damping_slot = jnp.repeat(damping_here, GMODES)[:, None, None]
    right_x = flow_x + TIME_STEP * (moment_x + forcing_slot * flow_x)
    right_y = flow_y + TIME_STEP * (moment_y + forcing_slot * flow_y)
    right_z = flow_z + TIME_STEP * (moment_z + forcing_slot * flow_z)
    right_b = buoyant + TIME_STEP * source_b
    wave_sq = wave_x * wave_x + wave_y * wave_y + wave_z * wave_z
    implicit = 1.0 + TIME_STEP * damping_slot * wave_sq
    rotation = TIME_STEP * CORIOLIS
    first_den = implicit * implicit + rotation * rotation
    second_den = implicit * implicit + TIME_STEP * TIME_STEP * BRUNT_SQUARED
    new_x = (implicit * right_x + rotation * right_y) / first_den
    new_y = (implicit * right_y - rotation * right_x) / first_den
    new_z = (implicit * right_z + TIME_STEP * right_b) / second_den
    new_b = (implicit * right_b - TIME_STEP * BRUNT_SQUARED * right_z) / second_den
    inverse_sq = 1.0 / (wave_sq + (wave_sq == 0).astype(jnp.float32))
    inner = (wave_x * new_x + wave_y * new_y + wave_z * new_z) * inverse_sq
    new_x = new_x - wave_x * inner
    new_y = new_y - wave_y * inner
    new_z = new_z - wave_z * inner
    return jnp.stack([new_x, new_y, new_z, new_b])


def solution(mesh):
    return jax.shard_map(
        shards,
        mesh=mesh,
        in_specs=(P(None, None, "grp", "slab", None), P(), P(), P(), P()),
        out_specs=P(None, None, "grp", "slab", None),
        check_vma=False,
    )
```

profile of v0, /device:TPU:0, one launch (start us, length us, event | category | flops | bytes accessed | tf_op | source)
XLA Modules:
  0.0 2021.2 jit_solution(9663195333022750134)
XLA Ops:
  15.7 7.3 fusion.4
  23.0 7.6 fusion.3
  30.6 10.1 subtract_bitcast_fusion.1
  40.7 10.2 add_bitcast_fusion.1
  50.9 12.4 pad_maximum_fusion.1
  63.3 27.2 %copy.46 = f32[7,2,64,16,256]{2,3,1,0,4:T(8,128)} copy(f32[7,2,64,16,256]{4,3,2,0,1:T(8,128)} %pad_maximum_fusion.1) | data formatting | bytes 29360128 | tf_op jit(solution)/shard_map/stack | solution.py:75
  90.5 37.7 %reshape.239 = f32[4,1,917504]{2,1,0:T(1,128)} reshape(f32[256,7,2,16,64]{4,3,2,1,0:T(8,128)} %bitcast.261) | data formatting | bytes 29360128
  128.2 172.1 %all_to_all.72 = f32[4,1,917504]{2,1,0:T(1,128)} all-to-all(f32[4,1,917504]{2,1,0:T(1,128)} %reshape.239), channel_id=1, replica_groups=mesh['grp'=4,'slab'=8] {'grp'}, dimensions={0} | all-to-all | bytes 29360128 | tf_op jit(solution)/shard_map/all_to_all | solution.py:85
  300.8 46.1 %reduce.2 = f32[4,917504]{1,0:T(4,128)} reduce(f32[4,1,917504]{2,1,0:T(1,128)} %all_to_all.72, f32[]{:T(128)} %broadcast.529), dimensions={1}, to_apply=%all_to_all.52.reduce_sub_computation | reduce | bytes 29360132 | tf_op jit(solution)/shard_map/all_to_all | solution.py:85
  346.9 42.0 %reshape.240 = f32[256,7,2,16,64]{4,3,2,1,0:T(8,128)} reshape(f32[4,917504]{1,0:T(4,128)} %reduce.2) | data formatting | bytes 29360128
  388.9 33.7 %copy.76 = f32[7,2,64,16,4,64]{2,4,5,3,0,1:T(4,128)} copy(f32[7,2,64,16,4,64]{2,3,1,0,5,4:T(8,128)} %bitcast.258) | data formatting | bytes 29360128 | tf_op jit(solution)/shard_map/all_to_all | solution.py:85
  422.6 26.9 %all_to_all.55 = f32[7,2,256,16,64]{2,4,3,0,1:T(8,128)} reshape(f32[7,2,4,64,16,64]{3,2,5,4,0,1:T(4,128)} %bitcast.259) | data formatting | bytes 29360128 | tf_op jit(solution)/shard_map/all_to_all | solution.py:85
  449.5 13.3 fusion.204
  462.8 12.8 fusion.99
  475.7 6.9 fusion.93
  482.6 10.2 fusion.95
  492.8 10.4 fusion.97
  503.2 10.5 subtract_bitcast_fusion
  513.7 8.4 add_bitcast_fusion
  522.1 13.1 pad_maximum_fusion.2
  535.2 27.2 %copy.48 = f32[7,2,256,16,64]{4,3,0,1,2:T(8,128)} copy(f32[7,2,256,16,64]{2,4,3,0,1:T(8,128)} %pad_maximum_fusion.2) | data formatting | bytes 29360128 | tf_op jit(solution)/shard_map/stack | solution.py:89
  562.4 23.1 %reshape.241 = f32[8,1,458752]{2,1,0:T(1,128)} reshape(f32[256,2,7,16,64]{4,3,2,1,0:T(8,128)} %bitcast.262) | data formatting | bytes 29360128
  585.5 5.6 all-to-all-start.1
  591.1 318.7 %all-to-all-done.1 = f32[8,1,458752]{2,1,0:T(1,128)} async-done(((f32[8,1,458752]{2,1,0:T(1,128)}), f32[8,1,458752]{2,1,0:T(1,128)}, u32[]{:S(2)}, u32[]{:S(2)}) %all-to-all-start.1) | async-done | bytes 14680096 | tf_op jit(solution)/shard_map/all_to_all | solution.py:90
  909.7 42.5 %reduce.3 = f32[8,458752]{1,0:T(8,128)} reduce(f32[8,1,458752]{2,1,0:T(1,128)} %all-to-all-done.1, f32[]{:T(128)} %broadcast.529), dimensions={1}, to_apply=%all_to_all.56.reduce_sub_computation | reduce | bytes 29360132 | tf_op jit(solution)/shard_map/all_to_all | solution.py:90
  952.2 26.2 %reshape.242 = f32[256,2,7,16,64]{4,3,2,1,0:T(8,128)} reshape(f32[8,458752]{1,0:T(8,128)} %reduce.3) | data formatting | bytes 29360128
  978.5 22.4 %copy.50 = f32[7,2,32,8,16,64]{5,4,3,2,1,0:T(8,128)} copy(f32[7,2,32,8,16,64]{5,4,0,1,2,3:T(8,128)} %bitcast.260) | data formatting | bytes 29360128 | tf_op jit(solution)/shard_map/all_to_all | solution.py:90
  1000.9 30.6 %fusion = f32[7,32,64,256]{3,2,1,0:T(8,128)} fusion(f32[7,2,32,128,64]{4,3,2,1,0:T(8,128)} %bitcast.256, f32[128]{0:T(128)S(1)} %fusion.119), kind=kOutput, calls=%fused_computation.3 | convolution fusion | flops 5637636096 | bytes 29360640 | tf_op jit(solution)/shard_map/fzky,kn->fzyn/dot_general | solution.py:91
  1031.5 32.3 %fusion.2 = f32[7,32,64,256]{3,2,1,0:T(8,128)} fusion(f32[7,32,64,256]{3,2,1,0:T(8,128)} %fusion, f32[7,2,32,128,64]{4,3,2,1,0:T(8,128)} %bitcast.257, f32[128]{0:T(128)S(1)} %fusion.119), kind=kOutput, calls=%fused_computation.12 | convolution fusion | flops 5641306112 | bytes 44040704 | tf_op jit(solution)/shard_map/fzky,kn->fzyn/dot_general | solution.py:91
  1068.3 4.9 subtract_dynamic-update-slice_fusion.1
  1076.0 11.5 convolution_bitcast_fusion
  1087.5 12.8 negate_bitcast_fusion
  1100.3 9.4 pad_maximum_fusion.3
  1109.7 23.4 %copy.53 = f32[6,2,32,128,64]{4,2,0,1,3:T(8,128)} copy(f32[6,2,32,128,64]{3,4,2,0,1:T(8,128)} %pad_maximum_fusion.3) | data formatting | bytes 25165824 | tf_op jit(solution)/shard_map/stack | solution.py:112
  1133.1 20.7 %reshape.243 = f32[8,1,393216]{2,1,0:T(1,128)} reshape(f32[128,2,6,32,64]{4,3,2,1,0:T(8,128)} %bitcast.264) | data formatting | bytes 25165824
  1153.8 280.5 %all_to_all.73 = f32[8,1,393216]{2,1,0:T(1,128)} all-to-all(f32[8,1,393216]{2,1,0:T(1,128)} %reshape.243), channel_id=1, replica_groups=mesh['grp'=4,'slab'=8] {'slab'}, dimensions={0} | all-to-all | bytes 25165824 | tf_op jit(solution)/shard_map/all_to_all | solution.py:113
  1434.2 36.7 %reduce.4 = f32[8,393216]{1,0:T(8,128)} reduce(f32[8,1,393216]{2,1,0:T(1,128)} %all_to_all.73, f32[]{:T(128)} %broadcast.529), dimensions={1}, to_apply=%all_to_all.60.reduce_sub_computation | reduce | bytes 25165828 | tf_op jit(solution)/shard_map/all_to_all | solution.py:113
  1470.9 22.6 %reshape.244 = f32[128,2,6,32,64]{4,3,2,1,0:T(8,128)} reshape(f32[8,393216]{1,0:T(8,128)} %reduce.4) | data formatting | bytes 25165824
  1493.5 28.3 %copy.55 = f32[6,2,8,32,16,64]{5,4,3,2,1,0:T(8,128)} copy(f32[6,2,8,32,16,64]{5,3,0,1,4,2:T(8,128)} %bitcast.265) | data formatting | bytes 25165824 | tf_op jit(solution)/shard_map/all_to_all | solution.py:113
  1521.8 18.0 fusion.203
  1539.8 10.8 copy.70
  1550.6 11.3 fusion.105
  1562.0 9.3 fusion.107
  1571.3 10.8 copy.71
  1582.1 11.5 fusion.109
  1593.5 6.2 fusion.103
  1599.8 6.9 add_bitcast_fusion.3
  1610.8 11.4 pad_maximum_fusion.4
  1622.2 23.4 %copy.58 = f32[6,2,256,16,64]{4,3,0,1,2:T(8,128)} copy(f32[6,2,256,16,64]{2,4,3,0,1:T(8,128)} %pad_maximum_fusion.4) | data formatting | bytes 25165824 | tf_op jit(solution)/shard_map/stack | solution.py:117
  1645.6 33.5 %reshape.245 = f32[4,1,786432]{2,1,0:T(1,128)} reshape(f32[256,2,6,16,64]{4,3,2,1,0:T(8,128)} %bitcast.266) | data formatting | bytes 25165824
  1679.1 6.3 all-to-all-start.3
  1694.4 14.5 psum.7
  1715.6 107.0 %all-to-all-done.3 = f32[4,1,786432]{2,1,0:T(1,128)} async-done(((f32[4,1,786432]{2,1,0:T(1,128)}), f32[4,1,786432]{2,1,0:T(1,128)}, u32[]{:S(2)}, u32[]{:S(2)}) %all-to-all-start.3) | async-done | bytes 12582944 | tf_op jit(solution)/shard_map/all_to_all | solution.py:118
  1822.6 40.1 %reduce.5 = f32[4,786432]{1,0:T(4,128)} reduce(f32[4,1,786432]{2,1,0:T(1,128)} %all-to-all-done.3, f32[]{:T(128)} %broadcast.529), dimensions={1}, to_apply=%all_to_all.64.reduce_sub_computation | reduce | bytes 25165828 | tf_op jit(solution)/shard_map/all_to_all | solution.py:118
  1862.7 31.9 %reshape.246 = f32[256,2,6,16,64]{4,3,2,1,0:T(8,128)} reshape(f32[4,786432]{1,0:T(4,128)} %reduce.5) | data formatting | bytes 25165824
  1894.6 30.2 %copy.77 = f32[6,2,4,64,16,64]{5,2,4,3,0,1:T(4,128)} copy(f32[6,2,4,64,16,64]{5,4,0,1,3,2:T(8,128)} %bitcast.267) | data formatting | bytes 25165824 | tf_op jit(solution)/shard_map/all_to_all | solution.py:118
  1924.9 23.2 %all_to_all.67 = f32[6,2,64,16,256]{4,3,2,0,1:T(8,128)} reshape(f32[6,2,64,16,4,64]{5,4,3,2,0,1:T(4,128)} %bitcast.268) | data formatting | bytes 25165824 | tf_op jit(solution)/shard_map/all_to_all | solution.py:118
  1948.1 9.6 fusion.8
  1957.7 6.3 fusion.7
  1963.9 6.6 add_bitcast_fusion.2
  1970.6 9.0 subtract_bitcast_fusion.2
  1979.6 8.9 maximum_multiply_fusion
  1992.5 9.3 add_divide_fusion.1
  2005.1 7.7 multiply_subtract_fusion.2
  (125 shorter events, 56.4 us)
Async XLA Ops:
  0.0 9.1 copy-start.17
  0.5 8.6 copy-start.22
  4.4 488.4 %copy-start.15 = (s32[256]{0:T(256)}, s32[256]{0:T(256)S(1)}, u32[]{:S(2)}) copy-start(s32[256]{0:T(256)S(1)} %get-tuple-element.6) | copy-start | bytes 3076
  5.0 4.2 copy-start.19
  9.7 2.2 slice-start
  10.1 3.2 slice-start.1
  462.8 12.9 copy-start.2
  462.8 19.8 slice-start.7
  475.7 6.9 slice-start.8
  585.5 324.3 %all-to-all-start.1 = ((f32[8,1,458752]{2,1,0:T(1,128)}), f32[8,1,458752]{2,1,0:T(1,128)}, u32[]{:S(2)}, u32[]{:S(2)}) async-start(f32[8,1,458752]{2,1,0:T(1,128)} %reshape.241), calls=%async_computation.1 | async-start | bytes 29360128 | tf_op jit(solution)/shard_map/all_to_all | solution.py:90
  1063.8 10.1 copy-start
  1539.8 10.8 copy-start.16
  1550.6 11.3 copy-start.4
  1582.1 11.5 copy-start.3
  1593.5 6.2 copy-start.6
  1599.8 6.9 copy-start.5
  1679.1 143.5 %all-to-all-start.3 = ((f32[4,1,786432]{2,1,0:T(1,128)}), f32[4,1,786432]{2,1,0:T(1,128)}, u32[]{:S(2)}, u32[]{:S(2)}) async-start(f32[4,1,786432]{2,1,0:T(1,128)} %reshape.245), calls=%async_computation.3 | async-start | bytes 25165824 | tf_op jit(solution)/shard_map/all_to_all | solution.py:118
  1685.4 23.5 %copy-start.24 = (f32[8]{0:T(128)S(1)}, f32[8]{0:T(128)}, u32[]{:S(2)}) copy-start(f32[8]{0:T(128)} %param.9) | copy-start | bytes 100
  1685.5 23.5 %copy-start.25 = (f32[8]{0:T(128)S(1)}, f32[8]{0:T(128)}, u32[]{:S(2)}) copy-start(f32[8]{0:T(128)} %param.8) | copy-start | bytes 100
  1685.5 23.7 %copy-start.21 = (s32[3]{0:T(128)S(1)}, s32[3]{0:T(128)}, u32[]{:S(2)}) copy-start(s32[3]{0:T(128)} %param.7) | copy-start | bytes 40
  1685.5 26.4 %copy-start.27 = (s32[64]{0:T(128)S(1)}, s32[64]{0:T(128)}, u32[]{:S(2)}) copy-start(s32[64]{0:T(128)} %get-tuple-element.12) | copy-start | bytes 772
  1685.5 26.5 %copy-start.26 = (f32[16]{0:T(128)S(1)}, f32[16]{0:T(128)}, u32[]{:S(2)}) copy-start(f32[16]{0:T(128)} %get-tuple-element.40) | copy-start | bytes 196
  1948.1 9.6 copy-start.1
  1979.6 8.9 copy-start.18
  1979.6 8.9 copy-start.20
  1979.6 8.9 copy-start.23
  1988.5 3.9 copy-start.7
  1988.5 3.9 copy-start.8
  1988.5 3.9 copy-start.9
  1988.5 4.0 copy-start.10
  1988.5 13.3 slice-start.2
  1992.1 9.8 slice-start.4
  1992.3 9.5 copy-start.11
  1992.3 9.5 copy-start.12
  1992.5 10.2 slice-start.3
  1992.5 11.4 slice-start.5
  1992.5 12.6 slice-start.6
  2012.8 3.5 copy-start.13
  2012.8 4.1 copy-start.14
where the time goes:
time: 2030 us; the launch traced here: 2020 us
  local copies, waits for them, and re-layouts  566 us (28%)
  blocking collectives  467 us (23%)
  waiting for transfers between devices  426 us (21%)
  other arithmetic  315 us (16%)
  matrix products  233 us (11%)
    all_to_all x1, waiting for transfers between devices, shards(): lax.all_to_all(grid_z, 'slab', split_axis=2, concat_axis=3, tiled=True)  319 us
    all_to_all x1, blocking collectives, shards(): lax.all_to_all(sectioned, 'slab', split_axis=3, concat_axis=2, tiled=True)  280 us
    unnamed x84, local copies, waits for them, and re-layouts  267 us
    all_to_all x1, blocking collectives, shards(): lax.all_to_all(spectral_y, 'grp', split_axis=4, concat_axis=2, tiled=True)  172 us
    all_to_all x1, waiting for transfers between devices, shards(): lax.all_to_all(spectral_z, 'grp', split_axis=2, concat_axis=4, tiled=True)  107 us
    unnamed x8, matrix products  78.6 us
    all_to_all x3, local copies, waits for them, and re-layouts, shards(): lax.all_to_all(spectral_y, 'grp', split_axis=4, concat_axis=2, tiled=True)  61.2 us
    all_to_all x2, local copies, waits for them, and re-layouts, shards(): lax.all_to_all(spectral_z, 'grp', split_axis=2, concat_axis=4, tiled=True)  53.4 us
  transfers between devices with their start and end apart: 2, of which 2 were waited for; matrix products, arithmetic and copies ran while one was open for 1% of the time, Pallas kernels for 0%

commit v1 on v0

--- a/solution.py
+++ b/solution.py
@@ -110,7 +110,9 @@
     )
     real_x, imag_x = x_forward(products, "fzyn,nk->fzky", cosine_xf, sine_xf)
     sectioned = jnp.stack([real_x, imag_x], axis=1)
-    pieces = lax.all_to_all(sectioned, "slab", split_axis=3, concat_axis=2, tiled=True)
+    parts = jnp.split(sectioned, lax.axis_size("slab"), axis=3)
+    received = lax.all_to_all(jnp.stack(parts), "slab", 0, 0)
+    pieces = jnp.concatenate(received, axis=2)
     real_part, imag_part = rotate(
         "fzxy,zs->fsxy", pieces[:, 0], pieces[:, 1], cosine_zf, sine_zf, True
     )

time: 2030 us -> 2130 us (1.049)
  local copies, waits for them, and re-layouts: 566 us -> 619 us
  other arithmetic: 315 us -> 361 us
    another operation x1 -> x9, local copies, waits for them, and re-layouts: 23.4 us -> 71.7 us  [shards(): received = lax.all_to_all(jnp.stack(parts), 'slab', 0, 0)]
    another operation x1, other arithmetic: 9.43 us -> 55.2 us  [shards(): received = lax.all_to_all(jnp.stack(parts), 'slab', 0, 0)]
    all_to_all x1 -> x0, local copies, waits for them, and re-layouts: 28.3 us -> none  [shards(): lax.all_to_all(sectioned, 'slab', split_axis=3, concat_axis=2, tiled=True)]
    unnamed x84 -> x103, local copies, waits for them, and re-layouts: 267 us -> 283 us
where the time goes in v1:
time: 2130 us; the launch traced here: 2120 us
  local copies, waits for them, and re-layouts  619 us (29%)
  blocking collectives  467 us (22%)
  waiting for transfers between devices  426 us (20%)
  other arithmetic  361 us (17%)
  matrix products  235 us (11%)
    all_to_all x1, waiting for transfers between devices, shards(): lax.all_to_all(grid_z, 'slab', split_axis=2, concat_axis=3, tiled=True)  319 us
    unnamed x103, local copies, waits for them, and re-layouts  283 us
    all_to_all x1, blocking collectives, shards(): received = lax.all_to_all(jnp.stack(parts), 'slab', 0, 0)  280 us
    all_to_all x1, blocking collectives, shards(): lax.all_to_all(spectral_y, 'grp', split_axis=4, concat_axis=2, tiled=True)  172 us
    all_to_all x1, waiting for transfers between devices, shards(): lax.all_to_all(spectral_z, 'grp', split_axis=2, concat_axis=4, tiled=True)  107 us
    unnamed x8, matrix products  81.2 us
    another operation x9, local copies, waits for them, and re-layouts, shards(): received = lax.all_to_all(jnp.stack(parts), 'slab', 0, 0)  71.7 us
    all_to_all x3, local copies, waits for them, and re-layouts, shards(): lax.all_to_all(spectral_y, 'grp', split_axis=4, concat_axis=2, tiled=True)  61.1 us
  transfers between devices with their start and end apart: 2, of which 2 were waited for; matrix products, arithmetic and copies ran while one was open for 1% of the time, Pallas kernels for 0%

profile of v1, /device:TPU:0, one launch (start us, length us, event | category | flops | bytes accessed | tf_op | source)
XLA Modules:
  0.0 2123.4 jit_solution(8792782294816858971)
XLA Ops:
  23.1 7.5 fusion.19
  30.6 10.1 add_bitcast_fusion.1
  40.7 10.3 subtract_bitcast_fusion.1
  50.9 12.4 pad_maximum_fusion.1
  63.3 27.2 %copy.50 = f32[7,2,64,16,256]{2,3,1,0,4:T(8,128)} copy(f32[7,2,64,16,256]{4,3,2,0,1:T(8,128)} %pad_maximum_fusion.1) | data formatting | bytes 29360128 | tf_op jit(solution)/shard_map/stack | solution.py:75
  90.5 37.7 %reshape.247 = f32[4,1,917504]{2,1,0:T(1,128)} reshape(f32[256,7,2,16,64]{4,3,2,1,0:T(8,128)} %bitcast.273) | data formatting | bytes 29360128
  128.2 172.0 %all_to_all.59 = f32[4,1,917504]{2,1,0:T(1,128)} all-to-all(f32[4,1,917504]{2,1,0:T(1,128)} %reshape.247), channel_id=1, replica_groups=mesh['grp'=4,'slab'=8] {'grp'}, dimensions={0} | all-to-all | bytes 29360128 | tf_op jit(solution)/shard_map/all_to_all | solution.py:85
  300.8 46.2 %reduce.2 = f32[4,917504]{1,0:T(4,128)} reduce(f32[4,1,917504]{2,1,0:T(1,128)} %all_to_all.59, f32[]{:T(128)} %broadcast.529), dimensions={1}, to_apply=%all_to_all.42.reduce_sub_computation | reduce | bytes 29360132 | tf_op jit(solution)/shard_map/all_to_all | solution.py:85
  347.0 41.8 %reshape.248 = f32[256,7,2,16,64]{4,3,2,1,0:T(8,128)} reshape(f32[4,917504]{1,0:T(4,128)} %reduce.2) | data formatting | bytes 29360128
  388.8 33.7 %copy.85 = f32[7,2,64,16,4,64]{2,4,5,3,0,1:T(4,128)} copy(f32[7,2,64,16,4,64]{2,3,1,0,5,4:T(8,128)} %bitcast.270) | data formatting | bytes 29360128 | tf_op jit(solution)/shard_map/all_to_all | solution.py:85
  422.4 26.9 %all_to_all.45 = f32[7,2,256,16,64]{2,4,3,0,1:T(8,128)} reshape(f32[7,2,4,64,16,64]{3,2,5,4,0,1:T(4,128)} %bitcast.271) | data formatting | bytes 29360128 | tf_op jit(solution)/shard_map/all_to_all | solution.py:85
  449.4 13.3 fusion.219
  462.7 11.1 fusion.112
  473.8 10.0 fusion.110
  483.8 10.4 fusion.108
  494.2 10.2 fusion.114
  504.4 10.4 subtract_bitcast_fusion
  514.8 8.4 add_bitcast_fusion
  523.2 13.1 pad_maximum_fusion.2
  536.3 27.2 %copy.52 = f32[7,2,256,16,64]{4,3,0,1,2:T(8,128)} copy(f32[7,2,256,16,64]{2,4,3,0,1:T(8,128)} %pad_maximum_fusion.2) | data formatting | bytes 29360128 | tf_op jit(solution)/shard_map/stack | solution.py:89
  563.5 23.1 %reshape.249 = f32[8,1,458752]{2,1,0:T(1,128)} reshape(f32[256,2,7,16,64]{4,3,2,1,0:T(8,128)} %bitcast.274) | data formatting | bytes 29360128
  592.1 318.7 %all-to-all-done.1 = f32[8,1,458752]{2,1,0:T(1,128)} async-done(((f32[8,1,458752]{2,1,0:T(1,128)}), f32[8,1,458752]{2,1,0:T(1,128)}, u32[]{:S(2)}, u32[]{:S(2)}) %all-to-all-start.1) | async-done | bytes 14680096 | tf_op jit(solution)/shard_map/all_to_all | solution.py:90
  910.8 42.5 %reduce.3 = f32[8,458752]{1,0:T(8,128)} reduce(f32[8,1,458752]{2,1,0:T(1,128)} %all-to-all-done.1, f32[]{:T(128)} %broadcast.529), dimensions={1}, to_apply=%all_to_all.46.reduce_sub_computation | reduce | bytes 29360132 | tf_op jit(solution)/shard_map/all_to_all | solution.py:90
  953.3 26.2 %reshape.250 = f32[256,2,7,16,64]{4,3,2,1,0:T(8,128)} reshape(f32[8,458752]{1,0:T(8,128)} %reduce.3) | data formatting | bytes 29360128
  979.5 22.4 %copy.54 = f32[7,2,32,8,16,64]{5,4,3,2,1,0:T(8,128)} copy(f32[7,2,32,8,16,64]{5,4,0,1,2,3:T(8,128)} %bitcast.272) | data formatting | bytes 29360128 | tf_op jit(solution)/shard_map/all_to_all | solution.py:90
  1001.9 30.6 %fusion = f32[7,32,64,256]{3,2,1,0:T(8,128)} fusion(f32[7,2,32,128,64]{4,3,2,1,0:T(8,128)} %bitcast.268, f32[128]{0:T(128)S(1)} %fusion.134), kind=kOutput, calls=%fused_computation.17 | convolution fusion | flops 5637636096 | bytes 29360640 | tf_op jit(solution)/shard_map/fzky,kn->fzyn/dot_general | solution.py:91
  1032.6 32.5 %fusion.17 = f32[7,32,64,256]{3,2,1,0:T(8,128)} fusion(f32[7,32,64,256]{3,2,1,0:T(8,128)} %fusion, f32[7,2,32,128,64]{4,3,2,1,0:T(8,128)} %bitcast.269, f32[128]{0:T(128)S(1)} %fusion.134), kind=kOutput, calls=%fused_computation.41 | convolution fusion | flops 5641306112 | bytes 44040704 | tf_op jit(solution)/shard_map/fzky,kn->fzyn/dot_general | solution.py:91
  1077.3 11.2 negate_bitcast_fusion
  1088.4 12.8 convolution_bitcast_fusion
  1101.2 55.2 %fusion.16 = (f32[1,6,2,32,16,64]{4,5,3,1,2,0:T(8,128)}, f32[1,6,2,32,16,64]{4,5,3,1,2,0:T(8,128)}, f32[1,6,2,32,16,64]{4,5,3,1,2,0:T(8,128)}, f32[1,6,2,32,16,6...) fusion(f32[6,1,32,128,64]{3,4,2,0,1:T(8,128)S(1)} %negate_bitca, ...), kind=kLoop, calls=%fused_computation.38 | loop fusion | flops 3145728 | bytes 25165824 | tf_op jit(solution)/shard_map/stack | solution.py:114
  1156.4 7.7 copy.64
  1164.1 8.8 copy.57
  1173.0 8.8 copy.58
  1181.8 8.9 copy.59
  1190.7 8.8 copy.60
  1199.5 8.8 copy.61
  1208.3 8.9 copy.62
  1217.2 8.8 copy.63
  1244.5 20.5 reshape.251
  1265.0 280.5 %all_to_all.60 = f32[8,1,393216]{2,1,0:T(1,128)} all-to-all(f32[8,1,393216]{2,1,0:T(1,128)} %reshape.251), channel_id=1, replica_groups=mesh['grp'=4,'slab'=8] {'slab'}, dimensions={0} | all-to-all | bytes 25165824 | tf_op jit(solution)/shard_map/all_to_all | solution.py:114
  1545.4 37.0 %reduce.4 = f32[8,393216]{1,0:T(8,128)} reduce(f32[8,1,393216]{2,1,0:T(1,128)} %all_to_all.60, f32[]{:T(128)} %broadcast.529), dimensions={1}, to_apply=%all_to_all.50.reduce_sub_computation | reduce | bytes 25165828 | tf_op jit(solution)/shard_map/all_to_all | solution.py:114
  1582.5 22.6 %reshape.252 = f32[8,6,2,32,16,64]{5,4,3,2,1,0:T(8,128)} reshape(f32[8,393216]{1,0:T(8,128)} %reduce.4) | data formatting | bytes 25165824
  1605.1 17.1 copy.65
  1622.2 18.0 fusion.218
  1640.3 11.0 copy.79
  1651.2 11.4 fusion.122
  1662.6 8.9 fusion.120
  1671.5 10.8 copy.80
  1682.3 10.3 fusion.118
  1692.7 8.9 fusion.124
  1712.6 11.4 pad_maximum_fusion.4
  1724.0 23.8 %copy.68 = f32[6,2,256,16,64]{4,3,0,1,2:T(8,128)} copy(f32[6,2,256,16,64]{2,4,3,0,1:T(8,128)} %pad_maximum_fusion.4) | data formatting | bytes 25165824 | tf_op jit(solution)/shard_map/stack | solution.py:119
  1747.8 33.3 %reshape.253 = f32[4,1,786432]{2,1,0:T(1,128)} reshape(f32[256,2,6,16,64]{4,3,2,1,0:T(8,128)} %bitcast.277) | data formatting | bytes 25165824
  1796.4 14.5 psum.7
  1817.7 107.0 %all-to-all-done.3 = f32[4,1,786432]{2,1,0:T(1,128)} async-done(((f32[4,1,786432]{2,1,0:T(1,128)}), f32[4,1,786432]{2,1,0:T(1,128)}, u32[]{:S(2)}, u32[]{:S(2)}) %all-to-all-start.3) | async-done | bytes 12582944 | tf_op jit(solution)/shard_map/all_to_all | solution.py:120
  1924.6 39.8 %reduce.5 = f32[4,786432]{1,0:T(4,128)} reduce(f32[4,1,786432]{2,1,0:T(1,128)} %all-to-all-done.3, f32[]{:T(128)} %broadcast.529), dimensions={1}, to_apply=%all_to_all.51.reduce_sub_computation | reduce | bytes 25165828 | tf_op jit(solution)/shard_map/all_to_all | solution.py:120
  1964.4 31.9 %reshape.254 = f32[256,2,6,16,64]{4,3,2,1,0:T(8,128)} reshape(f32[4,786432]{1,0:T(4,128)} %reduce.5) | data formatting | bytes 25165824
  1996.4 30.3 %copy.86 = f32[6,2,4,64,16,64]{5,2,4,3,0,1:T(4,128)} copy(f32[6,2,4,64,16,64]{5,4,0,1,3,2:T(8,128)} %bitcast.278) | data formatting | bytes 25165824 | tf_op jit(solution)/shard_map/all_to_all | solution.py:120
  2026.6 23.2 %all_to_all.54 = f32[6,2,64,16,256]{4,3,2,0,1:T(8,128)} reshape(f32[6,2,64,16,4,64]{5,4,3,2,0,1:T(4,128)} %bitcast.279) | data formatting | bytes 25165824 | tf_op jit(solution)/shard_map/all_to_all | solution.py:120
  2049.8 9.9 fusion.22
  2073.0 9.0 add_bitcast_fusion.2
  2082.1 8.9 maximum_multiply_fusion
  2095.0 9.3 add_divide_fusion.1
  2107.6 7.7 multiply_subtract_fusion.2
  (152 shorter events, 119.1 us)
Async XLA Ops:
  0.0 9.1 copy-start.23
  0.5 8.6 copy-start.28
  4.4 489.8 %copy-start.21 = (s32[256]{0:T(256)}, s32[256]{0:T(256)S(1)}, u32[]{:S(2)}) copy-start(s32[256]{0:T(256)S(1)} %get-tuple-element.6) | copy-start | bytes 3076
  5.0 4.2 copy-start.25
  9.7 2.2 slice-start
  10.1 3.2 slice-start.1
  462.7 11.1 copy-start.2
  462.7 21.1 slice-start.7
  473.7 10.1 slice-start.8
  586.5 324.2 %all-to-all-start.1 = ((f32[8,1,458752]{2,1,0:T(1,128)}), f32[8,1,458752]{2,1,0:T(1,128)}, u32[]{:S(2)}, u32[]{:S(2)}) async-start(f32[8,1,458752]{2,1,0:T(1,128)} %reshape.249), calls=%async_computation.1 | async-start | bytes 29360128 | tf_op jit(solution)/shard_map/all_to_all | solution.py:90
  1065.1 10.1 copy-start
  1226.0 3.9 copy-start.12
  1226.0 6.0 copy-start.11
  1229.9 4.2 copy-start.10
  1232.0 4.2 copy-start.9
  1234.1 4.1 copy-start.7
  1236.2 4.1 copy-start.8
  1640.3 11.0 copy-start.22
  1651.2 11.4 copy-start.4
  1682.3 10.3 copy-start.3
  1692.7 8.9 copy-start.6
  1701.6 6.9 copy-start.5
  1781.1 143.5 %all-to-all-start.3 = ((f32[4,1,786432]{2,1,0:T(1,128)}), f32[4,1,786432]{2,1,0:T(1,128)}, u32[]{:S(2)}, u32[]{:S(2)}) async-start(f32[4,1,786432]{2,1,0:T(1,128)} %reshape.253), calls=%async_computation.3 | async-start | bytes 25165824 | tf_op jit(solution)/shard_map/all_to_all | solution.py:120
  1790.2 20.7 copy-start.27
  1790.2 23.3 %copy-start.30 = (f32[8]{0:T(128)S(1)}, f32[8]{0:T(128)}, u32[]{:S(2)}) copy-start(f32[8]{0:T(128)} %param.9) | copy-start | bytes 100
  1790.2 23.3 %copy-start.31 = (f32[8]{0:T(128)S(1)}, f32[8]{0:T(128)}, u32[]{:S(2)}) copy-start(f32[8]{0:T(128)} %param.8) | copy-start | bytes 100
  1790.2 23.8 %copy-start.33 = (s32[64]{0:T(128)S(1)}, s32[64]{0:T(128)}, u32[]{:S(2)}) copy-start(s32[64]{0:T(128)} %get-tuple-element.12) | copy-start | bytes 772
  1790.2 23.9 %copy-start.32 = (f32[16]{0:T(128)S(1)}, f32[16]{0:T(128)}, u32[]{:S(2)}) copy-start(f32[16]{0:T(128)} %get-tuple-element.48) | copy-start | bytes 196
  2049.8 9.9 copy-start.1
  2082.0 8.9 copy-start.24
  2082.1 8.9 copy-start.26
  2082.1 8.9 copy-start.29
  2090.9 3.9 copy-start.13
  2091.0 3.9 copy-start.14
  2091.0 3.9 copy-start.15
  2091.0 4.0 copy-start.16
  2091.0 13.3 slice-start.2
  2094.6 9.8 slice-start.4
  2094.8 9.5 copy-start.17
  2094.8 9.5 copy-start.18
  2095.0 10.2 slice-start.3
  2095.0 11.4 slice-start.5
  2095.0 12.6 slice-start.6
  2115.3 3.5 copy-start.19
  2115.3 4.1 copy-start.20
